TPU v7x, 512 devices: a whole 4x8x8 slice. The times are simulated.
512 devices in a mesh: wide: 64 (over z_hi, y, core), narrow: 8 (over x, z_lo).
Axes of the slice: x: 4, y: 8, z: 8 (z_hi: 4, z_lo: 2; z = z_hi * 2 + z_lo), core: 2. Of those that a mesh axis runs over, the one named last changes fastest.
Arguments:
- enc_hidden: bfloat16 [12288, 6144], P('wide', 'narrow'), may hold values from -6 to 6
- enc_gain: float32 [6144], P('narrow'), may hold values from 0.1 to 1.9
- cross_weight: bfloat16 [6144, 256], P('narrow'), may hold values from -0.078125 to 0.078125
- assign: int32 [64], P('wide'), may hold values from 0 to 7
- token_ids: int32 [64, 2, 64], P('wide'), may hold values from 0 to 7999, as said below
- cross_table: bfloat16 [8000, 6144], P('wide', 'narrow'), may hold values from -540 to 540
- self_table: bfloat16 [8000, 6144], P('wide', 'narrow'), may hold values from -540 to 540
- kv_table: bfloat16 [8000, 256], P('wide'), may hold values from -6 to 6
- self_cache: bfloat16 [64, 64, 768, 256], P('wide', 'narrow'), may hold values from -6 to 6
Outputs:
- cross_out: bfloat16 [64, 2, 64, 6144], P('wide', None, None, 'narrow')
- self_out: bfloat16 [64, 2, 64, 6144], P('wide', None, 'narrow')
Inputs may be any that keep to these rules, and one draw needn't show every extreme that they name: `token_ids`: within one group, at most 4 of its 128 ids lie in any one of the 64 ranges of 125 consecutive ids, and some range holds exactly 4 of them.
All inputs are finite; a program needn't handle non-finite values.
Results may differ from a plain program's by a relative error of at most 0.009.
The roundings to bfloat16 on the way count: a program that leaves them out, or rounds other values in their place, can miss the bound.
Values may be sent and summed in bfloat16 or wider, within the bound.
No kernel may reach another device: no remote copies, remote signals or barrier semaphores. Data moves between devices by JAX's collectives and lax.ppermute only.
A program may use at most 64 MiB of HBM per device.

v0:
```python
import jax
import jax.numpy as jnp
from jax import lax
from jax.sharding import PartitionSpec as P

D = 6144
HEADS = 48
HEAD = 128
OWN = 8
ENC_LEN = 1536
EPS = 1e-06


def cut_along(shard, dim, length):
    shape = shard.shape
    pieces = shard.reshape(*shape[:dim], length, shape[dim] // length, *shape[dim + 1 :])
    return jnp.moveaxis(pieces, dim, 0)


def sent_and_summed(shard, axis, dim):
    pieces = cut_along(shard, dim, lax.axis_size(axis))
    arrived = lax.all_to_all(pieces, axis, split_axis=0, concat_axis=0, tiled=True)
    return arrived.sum(axis=0)


def sent_together(arrays, axis, dim, along):
    columns = [a.reshape(*a.shape[:along], -1) for a in arrays]
    both = jnp.concatenate(columns, axis=along)
    whole, at, outs = (sent_and_summed(both, axis, dim), 0, [])
    for a, column in zip(arrays, columns):
        piece = whole[..., at : at + column.shape[along]]
        outs.append(piece.reshape(*piece.shape[:along], *a.shape[along:]))
        at += column.shape[along]
    return tuple(outs)


def copy_for_each(shard, axis):
    length = lax.axis_size(axis)
    return lax.all_to_all(
        jnp.broadcast_to(shard[None], (length, *shard.shape)), axis, 0, 0, tiled=True
    )


def joined_along(pieces, dim):
    shape = list(pieces.shape[1:])
    shape[dim] *= pieces.shape[0]
    return jnp.moveaxis(pieces, 0, dim).reshape(shape)


def gather_directly(shard, axis, dim):
    pieces = copy_for_each(shard, axis)
    return joined_along(pieces, dim)


def in_one_piece(arrays, axis, split_dim, concat_dim, along):
    both = jnp.concatenate(arrays, axis=along)
    whole, at, outs = (
        lax.all_to_all(both, axis, split_axis=split_dim, concat_axis=concat_dim, tiled=True),
        0,
        [],
    )
    for a in arrays:
        outs.append(lax.slice_in_dim(whole, at, at + a.shape[along], axis=along))
        at += a.shape[along]
    return tuple(outs)


def body(
    enc_hidden,
    enc_gain,
    cross_weight,
    assign,
    token_ids,
    cross_table,
    self_table,
    kv_table,
    self_cache,
):
    hidden = enc_hidden.astype(jnp.float32)
    part_squares = jnp.sum(hidden * hidden, axis=1)
    scaled = (hidden * enc_gain).astype(jnp.bfloat16)
    part_proj = jnp.dot(scaled, cross_weight, preferred_element_type=jnp.float32)
    problem = assign[0]
    narrow_count = lax.axis_size("narrow")
    narrow_index = lax.axis_index("narrow")
    heads_dev = HEADS // narrow_count
    factor = HEAD ** (-0.5)
    projected, squares = sent_together((part_proj, part_squares), "narrow", 0, 1)
    enc_kv = (projected * lax.rsqrt(squares / D + EPS)[:, None]).astype(jnp.bfloat16)
    gathered = gather_directly(enc_kv, "wide", 0)
    span = ENC_LEN // narrow_count
    mine = lax.dynamic_slice_in_dim(gathered, problem * span, span, 0)
    mine = mine.reshape(OWN, span // OWN, 2 * HEAD)
    problem_kv = gather_directly(mine, "narrow", 1).reshape(ENC_LEN, 2 * HEAD)
    keys = problem_kv[:, :HEAD]
    values = problem_kv[:, HEAD:]
    wide_count = lax.axis_size("wide")
    per_owner = cross_table.shape[0]
    steps = token_ids.shape[1]
    cand = token_ids.shape[2]
    capacity = max(2, 2 * steps * cand // wide_count)
    flat = token_ids.reshape(-1)
    owner = flat // per_owner
    local = flat - owner * per_owner
    owner_hits = (owner[:, None] == jnp.arange(wide_count, dtype=jnp.int32)[None, :]).astype(
        jnp.int32
    )
    earlier = jnp.cumsum(owner_hits, axis=0) - owner_hits
    rank = jnp.sum(earlier * owner_hits, axis=1)
    target = owner * capacity + rank
    slot_match = target[None, :] == jnp.arange(wide_count * capacity, dtype=jnp.int32)[:, None]
    filled = jnp.any(slot_match, axis=1)
    request = jnp.where(filled, jnp.sum(jnp.where(slot_match, local[None, :], 0), axis=1), -1)
    asked = lax.all_to_all(
        request.reshape(wide_count, capacity), "wide", split_axis=0, concat_axis=0, tiled=True
    ).reshape(-1)
    valid = asked >= 0
    index = jnp.where(valid, asked, 0)

    def lookup(table):
        rows = jnp.take(table, index, axis=0)
        rows = jnp.where(valid[:, None], rows, jnp.zeros((), table.dtype))
        return rows.reshape(wide_count, capacity, table.shape[1])

    returned = in_one_piece(
        (lookup(cross_table), lookup(self_table), lookup(kv_table)), "wide", 0, 0, 2
    )
    cross_q, self_q, new_kv = [
        jnp.take(piece.reshape(wide_count * capacity, piece.shape[2]), target, axis=0)
        for piece in returned
    ]
    rows_total = steps * cand
    own_q = cross_q.reshape(rows_total, heads_dev, HEAD)
    scores = jnp.einsum("rhd,kd->rhk", own_q, keys, preferred_element_type=jnp.float32) * factor
    peak = jnp.max(scores, axis=-1, keepdims=True)
    expo = jnp.exp(scores - peak)
    total = jnp.sum(expo, axis=-1)
    result = (
        jnp.einsum(
            "rhk,kd->rhd", expo.astype(jnp.bfloat16), values, preferred_element_type=jnp.float32
        )
        / total[..., None]
    )
    cross_out = result.astype(jnp.bfloat16).reshape(1, steps, cand, heads_dev * HEAD)
    own_cand = cand // narrow_count
    queries = lax.all_to_all(
        self_q.reshape(steps, cand, self_q.shape[1]),
        "narrow",
        split_axis=1,
        concat_axis=2,
        tiled=True,
    )
    queries = queries.reshape(steps, own_cand, HEADS, HEAD)
    fresh = lax.dynamic_slice_in_dim(
        new_kv.reshape(steps, cand, new_kv.shape[1]), narrow_index * own_cand, own_cand, 1
    )
    cache = self_cache[0]
    prefix_scores = (
        jnp.einsum("tchd,cpd->tchp", queries, cache[..., :HEAD], preferred_element_type=jnp.float32)
        * factor
    )
    fresh_scores = (
        jnp.einsum("tchd,jcd->tchj", queries, fresh[..., :HEAD], preferred_element_type=jnp.float32)
        * factor
    )
    step_index = jnp.arange(steps, dtype=jnp.int32)
    allowed = (step_index[None, :] <= step_index[:, None])[:, None, None, :]
    fresh_masked = jnp.where(allowed, fresh_scores, -jnp.inf)
    peak = jnp.maximum(jnp.max(prefix_scores, axis=-1), jnp.max(fresh_masked, axis=-1))[..., None]
    prefix_expo = jnp.exp(prefix_scores - peak)
    fresh_expo = jnp.where(allowed, jnp.exp(fresh_masked - peak), 0.0)
    total = jnp.sum(prefix_expo, axis=-1) + jnp.sum(fresh_expo, axis=-1)
    summed = jnp.einsum(
        "tchp,cpd->tchd",
        prefix_expo.astype(jnp.bfloat16),
        cache[..., HEAD:],
        preferred_element_type=jnp.float32,
    )
    summed = summed + jnp.einsum(
        "tchj,jcd->tchd",
        fresh_expo.astype(jnp.bfloat16),
        fresh[..., HEAD:],
        preferred_element_type=jnp.float32,
    )
    self_result = summed / total[..., None]
    self_out = self_result.astype(jnp.bfloat16).reshape(1, steps, own_cand, HEADS * HEAD)
    return (cross_out, self_out)


def solution(mesh):
    placed = (
        P("wide", "narrow"),
        P("narrow"),
        P("narrow", None),
        P("wide"),
        P("wide", None, None),
        P("wide", "narrow"),
        P("wide", "narrow"),
        P("wide", None),
        P("wide", "narrow", None, None),
    )
    return jax.shard_map(
        body,
        mesh=mesh,
        in_specs=placed,
        out_specs=(P("wide", None, None, "narrow"), P("wide", None, "narrow", None)),
        check_vma=False,
    )
```

profile of v0, /device:TPU:24, one launch (start us, length us, event | category | flops | bytes accessed | tf_op | source)
XLA Modules:
  0.0 142.2 jit_solution(7858502208447242143)
XLA Ops:
  2.9 16.3 %all-to-all-start = ((s32[64,1,4]{2,1,0:T(1,128)}), s32[64,1,4]{2,1,0:T(1,128)S(1)}, u32[]{:S(2)}, u32[]{:S(2)}) async-start(s32[64,1,4]{2,1,0:T(1,128)} %bitcast), calls=%async_computation | async-start | bytes 65536 | tf_op jit(solution)/shard_map/all_to_all | solution.py:114
  19.3 1.1 fusion.27
  20.6 1.2 fusion.29
  22.6 6.0 %all-to-all-done = s32[64,1,4]{2,1,0:T(1,128)S(1)} async-done(((s32[64,1,4]{2,1,0:T(1,128)}), s32[64,1,4]{2,1,0:T(1,128)S(1)}, u32[]{:S(2)}, u32[]{:S(2)}) %all-to-all-start) | async-done | bytes 1056 | tf_op jit(solution)/shard_map/all_to_all | solution.py:114
  28.5 5.2 %all-to-all-start.2 = ((f32[8,24,257]{2,1,0:T(8,128)}), f32[8,24,257]{2,1,0:T(8,128)S(1)}, u32[]{:S(2)}, u32[]{:S(2)}) async-start(f32[8,24,257]{2,1,0:T(8,128)} %pad_maximum_fusion.1), calls=%async_computation.2 | async-start | bytes 589824 | tf_op jit(solution)/shard_map/all_to_all | solution.py:22
  35.3 1.2 gather_fusion
  36.5 1.2 gather_fusion.3
  37.7 1.2 gather_fusion.2
  39.5 1.3 pad_maximum_fusion
  41.4 7.2 %all-to-all-start.1 = ((bf16[64,4,1792]{2,1,0:T(4,128)(2,1)}), bf16[64,4,1792]{2,1,0:T(4,128)(2,1)S(1)}, u32[]{:S(2)}, u32[]{:S(2)}) async-start(bf16[64,4,1792]{2,1,0:T(4,128)(2,1)} %pad_maximum_fusion), calls=%async_computation.1 | async-start | bytes 1835008 | tf_op jit(solution)/shard_map/all_to_all | solution.py:58
  49.5 24.8 %all-to-all-done.1 = bf16[64,4,1792]{2,1,0:T(4,128)(2,1)S(1)} async-done(((bf16[64,4,1792]{2,1,0:T(4,128)(2,1)}), bf16[64,4,1792]{2,1,0:T(4,128)(2,1)S(1)}, u32[]{:S(2)}, u32[]{:S(2)}) %all-to-all-start.1) | async-done | bytes 917536 | tf_op jit(solution)/shard_map/all_to_all | solution.py:58
  74.4 0.9 broadcast_in_dim.142
  75.3 9.5 %all-to-all-start.3 = ((bf16[64,24,256]{2,1,0:T(8,128)(2,1)}), bf16[64,24,256]{2,1,0:T(8,128)(2,1)S(1)}, u32[]{:S(2)}, u32[]{:S(2)}) async-start(bf16[64,24,256]{2,1,0:T(8,128)(2,1)} %broadcast_in_dim.142), calls=%async_computation.3 | async-start | bytes 1572864 | tf_op jit(solution)/shard_map/all_to_all | solution.py:39
  89.4 18.6 %all-to-all-done.3 = bf16[64,24,256]{2,1,0:T(8,128)(2,1)S(1)} async-done(((bf16[64,24,256]{2,1,0:T(8,128)(2,1)}), bf16[64,24,256]{2,1,0:T(8,128)(2,1)S(1)}, u32[]{:S(2)}, u32[]{:S(2)}) %all-to-all-start.3) | async-done | bytes 786464 | tf_op jit(solution)/shard_map/all_to_all | solution.py:39
  108.0 4.8 %all-to-all-start.5 = ((bf16[2,64,768]{2,0,1:T(2,128)(2,1)}), bf16[2,64,768]{2,0,1:T(2,128)(2,1)S(1)}, u32[]{:S(2)}, u32[]{:S(2)}) async-start(bf16[2,64,768]{2,0,1:T(2,128)(2,1)} %copy.54), calls=%async_computation.5 | async-start | bytes 393216 | tf_op jit(solution)/shard_map/all_to_all | solution.py:146
  113.0 7.4 %all-to-all-done.5 = bf16[2,64,768]{2,0,1:T(2,128)(2,1)S(1)} async-done(((bf16[2,64,768]{2,0,1:T(2,128)(2,1)}), bf16[2,64,768]{2,0,1:T(2,128)(2,1)S(1)}, u32[]{:S(2)}, u32[]{:S(2)}) %all-to-all-start.5) | async-done | bytes 196640 | tf_op jit(solution)/shard_map/all_to_all | solution.py:146
  120.4 0.9 broadcast_in_dim.144
  121.3 3.7 %all-to-all-start.4 = ((bf16[8,8,24,256]{3,2,1,0:T(8,128)(2,1)}), bf16[8,8,24,256]{3,2,1,0:T(8,128)(2,1)S(1)}, u32[]{:S(2)}, u32[]{:S(2)}) async-start(bf16[8,8,24,256]{3,2,1,0:T(8,128)(2,1)} %broadcast_in_dim.144), calls=%async_computation.4 | async-start | bytes 1572864 | tf_op jit(solution)/shard_map/all_to_all | solution.py:39
  125.6 2.3 %bitcast_reduce_fusion = (f32[2,8,48]{2,0,1:T(2,128)S(1)}, f32[8,2,48,768]{3,2,1,0:T(8,128)S(1)}) fusion(bf16[2,8,48,128]{3,2,0,1:T(8,128)(2,1)S(1)} %reshape.320, bf16[8,768,256]{2,1,0:T(8,128)(2,1)} %bitcast.117), kind=kOutput, calls=%fused_computation.12 | convolution fusion | flops 152173824 | bytes 4131840 | tf_op jit(solution)/shard_map/tchd,cpd->tchp/dot_general | solution.py:159
  130.5 7.8 %all-to-all-done.4 = bf16[8,8,24,256]{3,2,1,0:T(8,128)(2,1)S(1)} async-done(((bf16[8,8,24,256]{3,2,1,0:T(8,128)(2,1)}), bf16[8,8,24,256]{3,2,1,0:T(8,128)(2,1)S(1)}, u32[]{:S(2)}, u32[]{:S(2)}) %all-to-all-start.4) | async-done | bytes 786464 | tf_op jit(solution)/shard_map/all_to_all | solution.py:39
  138.4 0.9 multiply_reduce_fusion
  139.3 0.9 fusion
  140.2 0.9 fusion.23
  141.3 0.9 reshape.317
  (81 shorter events, 14.1 us)
Async XLA Ops:
  0.6 20.0 %copy-start = (bf16[768,256]{1,0:T(8,128)(2,1)S(1)}, bf16[768,256]{1,0:T(8,128)(2,1)}, u32[]{:S(2)}) copy-start(bf16[768,256]{1,0:T(8,128)(2,1)} %param.15) | copy-start | bytes 1179652
  0.6 34.6 %copy-start.3 = (bf16[125,256]{1,0:T(8,128)(2,1)S(1)}, bf16[125,256]{1,0:T(8,128)(2,1)}, u32[]{:S(2)}) copy-start(bf16[125,256]{1,0:T(8,128)(2,1)} %param.20) | copy-start | bytes 192004
  0.7 35.8 %copy-start.1 = (bf16[125,768]{1,0:T(8,128)(2,1)S(1)}, bf16[125,768]{1,0:T(8,128)(2,1)}, u32[]{:S(2)}) copy-start(bf16[125,768]{1,0:T(8,128)(2,1)} %param.19) | copy-start | bytes 576004
  2.9 25.6 %all-to-all-start = ((s32[64,1,4]{2,1,0:T(1,128)}), s32[64,1,4]{2,1,0:T(1,128)S(1)}, u32[]{:S(2)}, u32[]{:S(2)}) async-start(s32[64,1,4]{2,1,0:T(1,128)} %bitcast), calls=%async_computation | async-start | bytes 65536 | tf_op jit(solution)/shard_map/all_to_all | solution.py:114
  28.5 12.8 %all-to-all-start.2 = ((f32[8,24,257]{2,1,0:T(8,128)}), f32[8,24,257]{2,1,0:T(8,128)S(1)}, u32[]{:S(2)}, u32[]{:S(2)}) async-start(f32[8,24,257]{2,1,0:T(8,128)} %pad_maximum_fusion.1), calls=%async_computation.2 | async-start | bytes 589824 | tf_op jit(solution)/shard_map/all_to_all | solution.py:22
  35.3 2.4 %copy-start.2 = (bf16[125,768]{1,0:T(8,128)(2,1)S(1)}, bf16[125,768]{1,0:T(8,128)(2,1)}, u32[]{:S(2)}) copy-start(bf16[125,768]{1,0:T(8,128)(2,1)} %param.18) | copy-start | bytes 576004
  40.8 44.0 %copy-start.5 = (s32[1,2,64]{2,1,0:T(2,128)S(1)}, s32[1,2,64]{2,1,0:T(2,128)}, u32[]{:S(2)}) copy-start(s32[1,2,64]{2,1,0:T(2,128)} %param.17) | copy-start | bytes 1540
  41.4 33.0 %all-to-all-start.1 = ((bf16[64,4,1792]{2,1,0:T(4,128)(2,1)}), bf16[64,4,1792]{2,1,0:T(4,128)(2,1)S(1)}, u32[]{:S(2)}, u32[]{:S(2)}) async-start(bf16[64,4,1792]{2,1,0:T(4,128)(2,1)} %pad_maximum_fusion), calls=%async_computation.1 | async-start | bytes 1835008 | tf_op jit(solution)/shard_map/all_to_all | solution.py:58
  75.3 32.7 %all-to-all-start.3 = ((bf16[64,24,256]{2,1,0:T(8,128)(2,1)}), bf16[64,24,256]{2,1,0:T(8,128)(2,1)S(1)}, u32[]{:S(2)}, u32[]{:S(2)}) async-start(bf16[64,24,256]{2,1,0:T(8,128)(2,1)} %broadcast_in_dim.142), calls=%async_computation.3 | async-start | bytes 1572864 | tf_op jit(solution)/shard_map/all_to_all | solution.py:39
  108.0 12.4 %all-to-all-start.5 = ((bf16[2,64,768]{2,0,1:T(2,128)(2,1)}), bf16[2,64,768]{2,0,1:T(2,128)(2,1)S(1)}, u32[]{:S(2)}, u32[]{:S(2)}) async-start(bf16[2,64,768]{2,0,1:T(2,128)(2,1)} %copy.54), calls=%async_computation.5 | async-start | bytes 393216 | tf_op jit(solution)/shard_map/all_to_all | solution.py:146
  121.3 17.0 %all-to-all-start.4 = ((bf16[8,8,24,256]{3,2,1,0:T(8,128)(2,1)}), bf16[8,8,24,256]{3,2,1,0:T(8,128)(2,1)S(1)}, u32[]{:S(2)}, u32[]{:S(2)}) async-start(bf16[8,8,24,256]{3,2,1,0:T(8,128)(2,1)} %broadcast_in_dim.144), calls=%async_computation.4 | async-start | bytes 1572864 | tf_op jit(solution)/shard_map/all_to_all | solution.py:39
  125.6 3.0 %copy-start.4 = (bf16[1,8,768,256]{3,2,1,0:T(8,128)(2,1)S(1)}, bf16[1,8,768,256]{3,2,1,0:T(8,128)(2,1)}, u32[]{:S(2)}) copy-start(bf16[1,8,768,256]{3,2,1,0:T(8,128)(2,1)} %param.21) | copy-start | bytes 9437188
where the time goes:
time: 143 us; the launch traced here: 142 us
  waiting for transfers between devices  65.2 us (46%)
  starting transfers between devices  46.7 us (33%)
  local copies, waits for them, and re-layouts  14.8 us (10%)
  other arithmetic  7.09 us (5%)
  matrix products  6.65 us (5%)
  between operations  1.74 us (1%)
    all_to_all x2, waiting for transfers between devices, copy_for_each(): lax.all_to_all(jnp.broadcast_to(shard[None], (length, *shard.shape)), axi...  26.4 us
    all_to_all x1, waiting for transfers between devices, in_one_piece(): lax.all_to_all(both, axis, split_axis=split_dim, concat_axis=concat_dim,...  24.8 us
    all_to_all x1, starting transfers between devices, body(): lax.all_to_all(request.reshape(wide_count, capacity), 'wide', split_axis=...  16.3 us
    all_to_all x2, starting transfers between devices, copy_for_each(): lax.all_to_all(jnp.broadcast_to(shard[None], (length, *shard.shape)), axi...  13.2 us
    all_to_all x1, waiting for transfers between devices, body(): lax.all_to_all(self_q.reshape(steps, cand, self_q.shape[1]), 'narrow', sp...  7.37 us
    all_to_all x1, starting transfers between devices, in_one_piece(): lax.all_to_all(both, axis, split_axis=split_dim, concat_axis=concat_dim,...  7.18 us
    all_to_all x1, waiting for transfers between devices, body(): lax.all_to_all(request.reshape(wide_count, capacity), 'wide', split_axis=...  5.97 us
    all_to_all x1, starting transfers between devices, sent_and_summed(): lax.all_to_all(pieces, axis, split_axis=0, concat_axis=0, tiled=True)  5.21 us
  transfers between devices with their start and end apart: 6, of which 6 were waited for; matrix products, arithmetic and copies ran while one was open for 14% of the time, Pallas kernels for 0%

commit v1 on v0

--- a/solution.py
+++ b/solution.py
@@ -2,6 +2,7 @@
 import jax.numpy as jnp
 from jax import lax
 from jax.sharding import PartitionSpec as P
+from jax.lax import all_to_all, axis_size
 
 D = 6144
 HEADS = 48
@@ -143,12 +144,19 @@
     )
     cross_out = result.astype(jnp.bfloat16).reshape(1, steps, cand, heads_dev * HEAD)
     own_cand = cand // narrow_count
-    queries = lax.all_to_all(
-        self_q.reshape(steps, cand, self_q.shape[1]),
-        "narrow",
-        split_axis=1,
-        concat_axis=2,
-        tiled=True,
+    queries = jnp.concatenate(
+        all_to_all(
+            jnp.stack(
+                jnp.split(
+                    self_q.reshape(steps, cand, self_q.shape[1]), axis_size("narrow"), axis=1
+                ),
+                axis=0,
+            ),
+            concat_axis=0,
+            axis_name="narrow",
+            split_axis=0,
+        ),
+        axis=2,
     )
     queries = queries.reshape(steps, own_cand, HEADS, HEAD)
     fresh = lax.dynamic_slice_in_dim(

time: 143 us -> 143 us (level)
  local copies, waits for them, and re-layouts: 14.8 us -> 18.8 us
  waiting for transfers between devices: 65.2 us -> 61.3 us
    unnamed x13 -> x20, local copies, waits for them, and re-layouts: 0.77 us -> 5.05 us
    all_to_all x2, waiting for transfers between devices: 26.4 us -> 22.8 us  [copy_for_each(): lax.all_to_all(jnp.broadcast_to(shard[None], (length, *shard.shape)), axi...]
  transfers between devices with their start and end apart: 6 -> 6, of which waited for: 6 -> 6; matrix products, arithmetic and copies ran while one was open for 14% -> 17% of each run, Pallas kernels for 0% -> 0%
where the time goes in v1:
time: 143 us; the launch traced here: 142 us
  waiting for transfers between devices  61.3 us (43%)
  starting transfers between devices  46.5 us (33%)
  local copies, waits for them, and re-layouts  18.8 us (13%)
  other arithmetic  7.08 us (5%)
  matrix products  6.64 us (5%)
  between operations  1.73 us (1%)
    all_to_all x1, waiting for transfers between devices, in_one_piece(): lax.all_to_all(both, axis, split_axis=split_dim, concat_axis=concat_dim,...  24.6 us
    all_to_all x2, waiting for transfers between devices, copy_for_each(): lax.all_to_all(jnp.broadcast_to(shard[None], (length, *shard.shape)), axi...  22.8 us
    all_to_all x1, starting transfers between devices, body(): lax.all_to_all(request.reshape(wide_count, capacity), 'wide', split_axis=...  16.3 us
    all_to_all x2, starting transfers between devices, copy_for_each(): lax.all_to_all(jnp.broadcast_to(shard[None], (length, *shard.shape)), axi...  13.1 us
    all_to_all x1, waiting for transfers between devices, body(): all_to_all(jnp.stack(jnp.split(self_q.reshape(steps, cand, self_q.shape[1...  7.37 us
    all_to_all x1, starting transfers between devices, in_one_piece(): lax.all_to_all(both, axis, split_axis=split_dim, concat_axis=concat_dim,...  7.18 us
    all_to_all x1, waiting for transfers between devices, body(): lax.all_to_all(request.reshape(wide_count, capacity), 'wide', split_axis=...  5.96 us
    all_to_all x1, starting transfers between devices, sent_and_summed(): lax.all_to_all(pieces, axis, split_axis=0, concat_axis=0, tiled=True)  5.21 us
  transfers between devices with their start and end apart: 6, of which 6 were waited for; matrix products, arithmetic and copies ran while one was open for 17% of the time, Pallas kernels for 0%

profile of v1, /device:TPU:24, one launch (start us, length us, event | category | flops | bytes accessed | tf_op | source)
XLA Modules:
  0.0 142.1 jit_solution(16929143206072249058)
XLA Ops:
  2.9 16.3 %all-to-all-start = ((s32[64,1,4]{2,1,0:T(1,128)}), s32[64,1,4]{2,1,0:T(1,128)S(1)}, u32[]{:S(2)}, u32[]{:S(2)}) async-start(s32[64,1,4]{2,1,0:T(1,128)} %bitcast), calls=%async_computation | async-start | bytes 65536 | tf_op jit(solution)/shard_map/all_to_all | solution.py:115
  19.3 1.1 fusion.27
  20.6 1.2 fusion.29
  22.6 6.0 %all-to-all-done = s32[64,1,4]{2,1,0:T(1,128)S(1)} async-done(((s32[64,1,4]{2,1,0:T(1,128)}), s32[64,1,4]{2,1,0:T(1,128)S(1)}, u32[]{:S(2)}, u32[]{:S(2)}) %all-to-all-start) | async-done | bytes 1056 | tf_op jit(solution)/shard_map/all_to_all | solution.py:115
  28.5 5.2 %all-to-all-start.2 = ((f32[8,24,257]{2,1,0:T(8,128)}), f32[8,24,257]{2,1,0:T(8,128)S(1)}, u32[]{:S(2)}, u32[]{:S(2)}) async-start(f32[8,24,257]{2,1,0:T(8,128)} %pad_maximum_fusion.1), calls=%async_computation.2 | async-start | bytes 589824 | tf_op jit(solution)/shard_map/all_to_all | solution.py:23
  35.3 1.2 gather_fusion
  36.5 1.2 gather_fusion.3
  37.7 1.2 gather_fusion.2
  39.5 1.3 pad_maximum_fusion
  41.4 7.2 %all-to-all-start.1 = ((bf16[64,4,1792]{2,1,0:T(4,128)(2,1)}), bf16[64,4,1792]{2,1,0:T(4,128)(2,1)S(1)}, u32[]{:S(2)}, u32[]{:S(2)}) async-start(bf16[64,4,1792]{2,1,0:T(4,128)(2,1)} %pad_maximum_fusion), calls=%async_computation.1 | async-start | bytes 1835008 | tf_op jit(solution)/shard_map/all_to_all | solution.py:59
  49.9 24.6 %all-to-all-done.1 = bf16[64,4,1792]{2,1,0:T(4,128)(2,1)S(1)} async-done(((bf16[64,4,1792]{2,1,0:T(4,128)(2,1)}), bf16[64,4,1792]{2,1,0:T(4,128)(2,1)S(1)}, u32[]{:S(2)}, u32[]{:S(2)}) %all-to-all-start.1) | async-done | bytes 917536 | tf_op jit(solution)/shard_map/all_to_all | solution.py:59
  74.5 0.9 broadcast_in_dim.142
  75.4 9.3 %all-to-all-start.3 = ((bf16[64,24,256]{2,1,0:T(8,128)(2,1)}), bf16[64,24,256]{2,1,0:T(8,128)(2,1)S(1)}, u32[]{:S(2)}, u32[]{:S(2)}) async-start(bf16[64,24,256]{2,1,0:T(8,128)(2,1)} %broadcast_in_dim.142), calls=%async_computation.3 | async-start | bytes 1572864 | tf_op jit(solution)/shard_map/all_to_all | solution.py:40
  92.9 15.0 %all-to-all-done.3 = bf16[64,24,256]{2,1,0:T(8,128)(2,1)S(1)} async-done(((bf16[64,24,256]{2,1,0:T(8,128)(2,1)}), bf16[64,24,256]{2,1,0:T(8,128)(2,1)S(1)}, u32[]{:S(2)}, u32[]{:S(2)}) %all-to-all-start.3) | async-done | bytes 786464 | tf_op jit(solution)/shard_map/all_to_all | solution.py:40
  107.9 4.7 %all-to-all-start.5 = ((bf16[8,2,8,768]{3,2,1,0:T(8,128)(2,1)}), bf16[8,2,8,768]{3,2,1,0:T(8,128)(2,1)S(1)}, u32[]{:S(2)}, u32[]{:S(2)}) async-start(bf16[8,2,8,768]{3,2,1,0:T(8,128)(2,1)} %fusion.34), calls=%async_computation.5 | async-start | bytes 393216 | tf_op jit(solution)/shard_map/all_to_all | solution.py:148
  112.9 7.4 %all-to-all-done.5 = bf16[8,2,8,768]{3,2,1,0:T(8,128)(2,1)S(1)} async-done(((bf16[8,2,8,768]{3,2,1,0:T(8,128)(2,1)}), bf16[8,2,8,768]{3,2,1,0:T(8,128)(2,1)S(1)}, u32[]{:S(2)}, u32[]{:S(2)}) %all-to-all-start.5) | async-done | bytes 196640 | tf_op jit(solution)/shard_map/all_to_all | solution.py:148
  120.3 0.9 broadcast_in_dim.144
  121.2 3.7 %all-to-all-start.4 = ((bf16[8,8,24,256]{3,2,1,0:T(8,128)(2,1)}), bf16[8,8,24,256]{3,2,1,0:T(8,128)(2,1)S(1)}, u32[]{:S(2)}, u32[]{:S(2)}) async-start(bf16[8,8,24,256]{3,2,1,0:T(8,128)(2,1)} %broadcast_in_dim.144), calls=%async_computation.4 | async-start | bytes 1572864 | tf_op jit(solution)/shard_map/all_to_all | solution.py:40
  125.5 2.3 %bitcast_reduce_fusion = (f32[2,8,48]{2,0,1:T(2,128)S(1)}, f32[8,2,48,768]{3,2,1,0:T(8,128)S(1)}) fusion(bf16[2,8,48,128]{3,2,0,1:T(8,128)(2,1)S(1)} %reshape_reshape.7, bf16[8,768,256]{2,1,0:T(8,128)(2,1)} %bitcast.152), kind=kOutput, calls=%fused_computation.12 | convolution fusion | flops 152173824 | bytes 4131840 | tf_op jit(solution)/shard_map/tchd,cpd->tchp/dot_general | solution.py:167
  130.4 7.9 %all-to-all-done.4 = bf16[8,8,24,256]{3,2,1,0:T(8,128)(2,1)S(1)} async-done(((bf16[8,8,24,256]{3,2,1,0:T(8,128)(2,1)}), bf16[8,8,24,256]{3,2,1,0:T(8,128)(2,1)S(1)}, u32[]{:S(2)}, u32[]{:S(2)}) %all-to-all-start.4) | async-done | bytes 786464 | tf_op jit(solution)/shard_map/all_to_all | solution.py:40
  138.3 0.9 multiply_reduce_fusion
  139.2 0.9 fusion
  140.1 0.9 fusion.23
  141.2 0.9 reshape.316
  (86 shorter events, 18.1 us)
Async XLA Ops:
  0.6 20.0 %copy-start = (bf16[768,256]{1,0:T(8,128)(2,1)S(1)}, bf16[768,256]{1,0:T(8,128)(2,1)}, u32[]{:S(2)}) copy-start(bf16[768,256]{1,0:T(8,128)(2,1)} %param.15) | copy-start | bytes 1179652
  0.6 34.6 %copy-start.3 = (bf16[125,256]{1,0:T(8,128)(2,1)S(1)}, bf16[125,256]{1,0:T(8,128)(2,1)}, u32[]{:S(2)}) copy-start(bf16[125,256]{1,0:T(8,128)(2,1)} %param.20) | copy-start | bytes 192004
  0.7 35.8 %copy-start.1 = (bf16[125,768]{1,0:T(8,128)(2,1)S(1)}, bf16[125,768]{1,0:T(8,128)(2,1)}, u32[]{:S(2)}) copy-start(bf16[125,768]{1,0:T(8,128)(2,1)} %param.19) | copy-start | bytes 576004
  2.9 25.6 %all-to-all-start = ((s32[64,1,4]{2,1,0:T(1,128)}), s32[64,1,4]{2,1,0:T(1,128)S(1)}, u32[]{:S(2)}, u32[]{:S(2)}) async-start(s32[64,1,4]{2,1,0:T(1,128)} %bitcast), calls=%async_computation | async-start | bytes 65536 | tf_op jit(solution)/shard_map/all_to_all | solution.py:115
  28.5 12.8 %all-to-all-start.2 = ((f32[8,24,257]{2,1,0:T(8,128)}), f32[8,24,257]{2,1,0:T(8,128)S(1)}, u32[]{:S(2)}, u32[]{:S(2)}) async-start(f32[8,24,257]{2,1,0:T(8,128)} %pad_maximum_fusion.1), calls=%async_computation.2 | async-start | bytes 589824 | tf_op jit(solution)/shard_map/all_to_all | solution.py:23
  35.3 2.4 %copy-start.2 = (bf16[125,768]{1,0:T(8,128)(2,1)S(1)}, bf16[125,768]{1,0:T(8,128)(2,1)}, u32[]{:S(2)}) copy-start(bf16[125,768]{1,0:T(8,128)(2,1)} %param.18) | copy-start | bytes 576004
  39.4 9.9 %copy-start.5 = (s32[1,2,64]{2,1,0:T(2,128)S(1)}, s32[1,2,64]{2,1,0:T(2,128)}, u32[]{:S(2)}) copy-start(s32[1,2,64]{2,1,0:T(2,128)} %param.17) | copy-start | bytes 1540
  41.4 33.1 %all-to-all-start.1 = ((bf16[64,4,1792]{2,1,0:T(4,128)(2,1)}), bf16[64,4,1792]{2,1,0:T(4,128)(2,1)S(1)}, u32[]{:S(2)}, u32[]{:S(2)}) async-start(bf16[64,4,1792]{2,1,0:T(4,128)(2,1)} %pad_maximum_fusion), calls=%async_computation.1 | async-start | bytes 1835008 | tf_op jit(solution)/shard_map/all_to_all | solution.py:59
  75.4 32.5 %all-to-all-start.3 = ((bf16[64,24,256]{2,1,0:T(8,128)(2,1)}), bf16[64,24,256]{2,1,0:T(8,128)(2,1)S(1)}, u32[]{:S(2)}, u32[]{:S(2)}) async-start(bf16[64,24,256]{2,1,0:T(8,128)(2,1)} %broadcast_in_dim.142), calls=%async_computation.3 | async-start | bytes 1572864 | tf_op jit(solution)/shard_map/all_to_all | solution.py:40
  107.9 12.4 %all-to-all-start.5 = ((bf16[8,2,8,768]{3,2,1,0:T(8,128)(2,1)}), bf16[8,2,8,768]{3,2,1,0:T(8,128)(2,1)S(1)}, u32[]{:S(2)}, u32[]{:S(2)}) async-start(bf16[8,2,8,768]{3,2,1,0:T(8,128)(2,1)} %fusion.34), calls=%async_computation.5 | async-start | bytes 393216 | tf_op jit(solution)/shard_map/all_to_all | solution.py:148
  121.2 17.0 %all-to-all-start.4 = ((bf16[8,8,24,256]{3,2,1,0:T(8,128)(2,1)}), bf16[8,8,24,256]{3,2,1,0:T(8,128)(2,1)S(1)}, u32[]{:S(2)}, u32[]{:S(2)}) async-start(bf16[8,8,24,256]{3,2,1,0:T(8,128)(2,1)} %broadcast_in_dim.144), calls=%async_computation.4 | async-start | bytes 1572864 | tf_op jit(solution)/shard_map/all_to_all | solution.py:40
  125.5 3.0 %copy-start.4 = (bf16[1,8,768,256]{3,2,1,0:T(8,128)(2,1)S(1)}, bf16[1,8,768,256]{3,2,1,0:T(8,128)(2,1)}, u32[]{:S(2)}) copy-start(bf16[1,8,768,256]{3,2,1,0:T(8,128)(2,1)} %param.21) | copy-start | bytes 9437188
